TPU v7x, 128 devices: a whole 4x4x4 slice. The times are simulated.
128 devices in a mesh: node: 8 (over z_hi, x), row: 16 (over y, z_lo, core).
Axes of the slice: x: 4, y: 4, z: 4 (z_hi: 2, z_lo: 2; z = z_hi * 2 + z_lo), core: 2. Of those that a mesh axis runs over, the one named last changes fastest.
Arguments:
- inputs: float32 [16, 64, 128, 128], P(None, 'row'), may hold values from -8 to 8
- diagonal: float32 [64, 128, 128], P('row'), may hold values from 0.05 to 1
- observations: float32 [16, 64, 128, 128], P(None, 'row'), may hold values from -0.005859375 to 0.005859375
- frequencies: float32 [8], replicated, may hold values from 0.2 to 3
- weights: float32 [8], replicated, may hold values from 0.5 to 2
- counts: int32 [8], replicated, may hold values from 3 to 6, as said below
- assignment: int32 [8], replicated, may hold values from 0 to 7, each once
Outputs:
- probe_response: float32 [16, 64, 128, 128], P(None, 'row')
- group_gram: float32 [8, 16, 16], P('node')
Inputs may be any that keep to these rules, and one draw needn't show every extreme that they name: `counts`: some node has 6 sweeps and some node 3 in every draw. `assignment`: each node 0 to 7 appears once.
All inputs are finite; a program needn't handle non-finite values.
Results may differ from a plain program's by a relative error of at most 0.0003.
Values sent between devices are 32-bit elements; how exact they have to be, the bound alone decides.
No kernel may reach another device: no remote copies, remote signals or barrier semaphores. Data moves between devices by JAX's collectives and lax.ppermute only.
A program may use at most 192 MiB of HBM per device.

v0:
```python
import jax
import jax.numpy as jnp
from jax import lax
from jax.experimental import pallas as pl
from jax.experimental.pallas import tpu as pltpu
from jax.sharding import PartitionSpec as P

QUAD = 8
COLS = 16
DEPTH = 5
PLANES = 4
ROWS = 16
WIDE = ROWS + 2 * DEPTH
SPAN = PLANES + 2 * DEPTH
LANES = 128
CELLS = 1048576.0
SEND_B = sum(WIDE - 2 * d for d in range(1, PLANES + 1)) * COLS
SEND_E = PLANES * 24
FAR_B = ROWS * COLS
OWN_B = PLANES * WIDE * COLS
STEP = 8
PART = 2048
PACK_LIMIT = 50 << 20
SOLVE_LIMIT = 51 << 20
F32 = jnp.float32
BF16 = jnp.bfloat16
VMEM = pl.BlockSpec(memory_space=pltpu.VMEM)
SMEM = pl.BlockSpec(memory_space=pltpu.SMEM)
ANY = pl.BlockSpec(memory_space=pl.ANY)


def window_copies(src_ref, start, dst_ref, sems):
    rows = pl.ds(pl.multiple_of(start, 8), 32)
    return [
        pltpu.make_async_copy(
            src_ref.at[pl.ds(2 * i, 2), :, rows, :], dst_ref.at[pl.ds(2 * i, 2)], sems.at[i]
        )
        for i in range(COLS // 2)
    ]


def first_row(at):
    return jnp.clip(at - 8, 0, 96)


def fill_edge(edge_ref, diag_ref):
    for x in range(PLANES):
        edge_ref[x, pl.ds(0, 16), :] = jnp.zeros((16, LANES), F32)
        edge_ref[x, pl.ds(144, 16), :] = jnp.zeros((16, LANES), F32)
        edge_ref[x, pl.ds(16, 128), :] = diag_ref[x] + 6.0


def turned_rows(dst_ref, base, flat_ref, offset, first, count):
    for q in range(count):
        y = jnp.clip(first + q, 0, 127) + offset
        dst_ref[pl.ds(base + q * COLS, COLS), :] = flat_ref[
            pl.ds(y, COLS, stride=PLANES * 32), :
        ]


def pack_kernel(
    at_ref, src_ref, diag_hbm, pair_ref, cross_ref, even_ref, odd_ref, edge_ref, diag_ref, win, sems
):
    mine = at_ref[0]
    other = jnp.where(mine >= 64, mine - 64, mine + 64)
    whole = pltpu.make_async_copy(diag_hbm, diag_ref, sems.at[2, 0])
    whole.start()
    copies = []
    for w, t in enumerate((mine, other)):
        copies += window_copies(src_ref, first_row(t), win.at[w], sems.at[w])
    for c in copies:
        c.start()
    whole.wait()
    fill_edge(edge_ref, diag_ref)
    for c in copies:
        c.wait()
    flat = win.reshape(2 * COLS * PLANES * 32, LANES)

    def send(dst_ref, base, at, plane, d, count):
        offset = jnp.where(at == mine, 0, COLS * PLANES * 32) + plane * 32 - first_row(at)
        turned_rows(dst_ref, base, flat, offset, at - DEPTH + d, count)

    core, odd = at_ref[2], at_ref[3]
    base = 0
    for d in range(1, PLANES + 1):
        count = WIDE - 2 * d
        for dst_ref, at, right in ((pair_ref, mine, core == 0), (cross_ref, at_ref[1], core == 1)):
            plane = jnp.where(right, PLANES - d, d - 1)
            send(dst_ref, base, at, plane, d, count)
            dst_ref[pl.ds(SEND_B + (d - 1) * 24, 24), :] = edge_ref[
                plane, pl.ds(16 + at - DEPTH + d, 24), :
            ]
        base += count * COLS
    for dst_ref, at, right in ((even_ref, mine, odd == 0), (odd_ref, other, odd == 1)):
        plane = jnp.where(right, PLANES - 1, 0)
        send(dst_ref, 0, at, plane, DEPTH, ROWS)
        dst_ref[pl.ds(FAR_B, ROWS), :] = edge_ref[plane, pl.ds(16 + at, ROWS), :]


def pack(at, inputs, diagonal):
    out = lambda n: jax.ShapeDtypeStruct((n, LANES), F32)
    return pl.pallas_call(
        pack_kernel,
        out_shape=(
            out(SEND_B + SEND_E),
            out(SEND_B + SEND_E),
            out(FAR_B + ROWS),
            out(FAR_B + ROWS),
        ),
        in_specs=[SMEM, ANY, ANY],
        out_specs=(VMEM,) * 4,
        scratch_shapes=[
            pltpu.VMEM((PLANES, 160, LANES), F32),
            pltpu.VMEM((PLANES, 128, LANES), F32),
            pltpu.VMEM((2, COLS, PLANES, 32, LANES), F32),
            pltpu.SemaphoreType.DMA((3, 8)),
        ],
        compiler_params=pltpu.CompilerParams(vmem_limit_bytes=PACK_LIMIT),
        name="pack",
    )(at, inputs, diagonal)


def prep_kernel(at_ref, src_ref, diag_ref, obs_ref, after_ref, own_ref, probe_ref, edge_ref, win, obs, sems):
    mine = at_ref[0]
    copies = window_copies(src_ref, first_row(mine), win, sems)
    copies.append(
        pltpu.make_async_copy(
            obs_ref.at[:, :, pl.ds(pl.multiple_of(mine, 16), ROWS), :], obs, sems.at[8]
        )
    )
    for c in copies:
        c.start()
    fill_edge(edge_ref, diag_ref)
    for c in copies:
        c.wait()
    flat = win.reshape(COLS * PLANES * 32, LANES)
    seen = obs.reshape(COLS * PLANES * ROWS, LANES)
    for x in range(PLANES):
        offset = x * 32 - first_row(mine)
        turned_rows(own_ref, x * WIDE * COLS, flat, offset, mine - DEPTH, WIDE)
        own_ref[pl.ds(OWN_B + x * 32, 32), :] = edge_ref[x, pl.ds(16 + mine - DEPTH, 32), :]
        for y in range(ROWS):
            v = seen[pl.ds(x * ROWS + y, COLS, stride=PLANES * ROWS), :]
            hi = v.astype(BF16)
            at = pl.ds((x * ROWS + y) * LANES, LANES)
            probe_ref[0:16, at] = hi
            probe_ref[16:32, at] = (v - hi.astype(F32)).astype(BF16)


def prep(at, inputs, diagonal, observations, after):
    return pl.pallas_call(
        prep_kernel,
        out_shape=(
            jax.ShapeDtypeStruct((OWN_B + PLANES * 32, LANES), F32),
            jax.ShapeDtypeStruct((32, PLANES * ROWS * LANES), BF16),
        ),
        in_specs=[SMEM, ANY, VMEM, ANY, ANY],
        out_specs=(VMEM, VMEM),
        scratch_shapes=[
            pltpu.VMEM((PLANES, 160, LANES), F32),
            pltpu.VMEM((COLS, PLANES, 32, LANES), F32),
            pltpu.VMEM((COLS, PLANES, ROWS, LANES), F32),
            pltpu.SemaphoreType.DMA((9,)),
        ],
        compiler_params=pltpu.CompilerParams(vmem_limit_bytes=PACK_LIMIT),
        cost_estimate=pl.CostEstimate(flops=40_000_000, bytes_accessed=4_000_000, transcendentals=0),
        name="prep",
    )(at, inputs, diagonal, observations, after)


def solve_kernel(
    at_ref, freq_ref, count_ref, own_ref, pair_ref, cross_ref, even_ref, odd_ref, probe_ref,
    full_ref, part_ref,
    src, even, odd, near, edge, gre, gim, cat, stage, sems, out_sem,
):
    core, half_odd = at_ref[2], at_ref[3]

    def ghost(s, d):
        if d < DEPTH:
            right = core == s
        else:
            right = half_odd == s
        return jnp.where(right, DEPTH + PLANES - 1 + d, DEPTH - d)

    def start():
        copies = []

        def fetch(a, b):
            copies.append(pltpu.make_async_copy(a, b, sems.at[len(copies)]))
            copies[-1].start()

        fetch(probe_ref, cat.at[pl.ds(64, 32)])
        for x in range(PLANES):
            fetch(
                own_ref.at[pl.ds(x * WIDE * COLS, WIDE * COLS)],
                src.at[DEPTH + x],
            )
        fetch(own_ref.at[pl.ds(OWN_B, PLANES * 32)], stage.at[pl.ds(0, 128)])
        for s, (close, far) in enumerate(((pair_ref, even_ref), (cross_ref, odd_ref))):
            base = 0
            for d in range(1, PLANES + 1):
                count = (WIDE - 2 * d) * COLS
                fetch(close.at[pl.ds(base, count)], src.at[ghost(s, d), pl.ds(d * COLS, count)])
                base += count
            fetch(far.at[pl.ds(0, FAR_B)], src.at[ghost(s, DEPTH), pl.ds(DEPTH * COLS, FAR_B)])
            fetch(close.at[pl.ds(SEND_B, SEND_E)], stage.at[pl.ds(128 + s * 112, SEND_E)])
            fetch(far.at[pl.ds(FAR_B, ROWS)], stage.at[pl.ds(128 + s * 112 + 96, ROWS)])
        edge[...] = jnp.zeros_like(edge)
        part_ref[...] = jnp.zeros_like(part_ref)
        apart = lax.broadcasted_iota(jnp.int32, (LANES, LANES), 0) - lax.broadcasted_iota(
            jnp.int32, (LANES, LANES), 1
        )
        ones = jnp.where(jnp.abs(apart) == 1, 1.0, 0.0).astype(BF16)
        near[0:LANES, :] = ones
        near[LANES : 2 * LANES, :] = ones
        for c in copies:
            c.wait()
        for x in range(PLANES):
            edge[DEPTH + x] = stage[pl.ds(x * 32, 32), :]
        for s in range(2):
            for d in range(1, DEPTH + 1):
                edge[ghost(s, d), pl.ds(d, WIDE - 2 * d), :] = stage[
                    pl.ds(128 + s * 112 + (d - 1) * 24, WIDE - 2 * d), :
                ]

    def leaving(node):
        return [
            pltpu.make_async_copy(
                cat.at[pl.ds(64 * i, 64)],
                full_ref.at[pl.ds(pl.multiple_of(64 * node + 64 * i, 8), 64)],
                out_sem.at[i],
            )
            for i in range(1)
        ]

    start()

    @pl.loop(0, QUAD)
    def _(node):
        count = count_ref[node]
        freq = freq_ref[node]

        for px in range(SPAN):
            d = edge[px]
            inv = 1.0 / (d * d + freq * freq)
            gre[px] = d * inv
            gim[px] = jnp.where(d > 0.0, -freq * inv, 0.0)

        def planes(level, top, m, body):
            dd = level - m
            idle = (dd < 0) | (level > top)
            trips = jnp.where(idle, 0, jnp.where(dd == 0, PLANES // 2, 1))

            @pl.loop(0, trips)
            def _(q):
                left = jnp.where(dd == 0, DEPTH + 2 * q, DEPTH - dd)
                right = jnp.where(dd == 0, left + 1, DEPTH + PLANES - 1 + dd)
                body(left, right)

        def spread(ref, px, r):
            return jnp.broadcast_to(ref[px, pl.ds(r, 1), :], (COLS, LANES))

        def at_row(r):
            return pl.ds(r * COLS, COLS)

        def halves(v):
            hi = v.astype(BF16)
            return hi, (v - hi.astype(F32)).astype(BF16)

        def begin(field):
            for m in range(DEPTH + 1):

                def first(*pair_of, m=m):
                    for px in pair_of:
                        for r in range(DEPTH - m, DEPTH + ROWS + m):
                            b = src[px, at_row(r), :]
                            field[0, px, at_row(r), :] = spread(gre, px, r) * b
                            field[1, px, at_row(r), :] = spread(gim, px, r) * b

                planes(count - 1, count - 1, m, first)

        def sweep(old, emit, group, m):
            start, rows = DEPTH - m, ROWS + 2 * m
            beside = []
            for px in group:
                lhs = []
                for i in range(rows):
                    for c in range(2):
                        hi, lo = halves(old[c, px, at_row(start + i), :])
                        lhs.append(jnp.concatenate([hi, lo], 1))
                beside.append(
                    jnp.dot(jnp.concatenate(lhs, 0), near[...], preferred_element_type=F32)
                )
            for px, side in zip(group, beside):

                def get(c, p, r):
                    return old[c, p, at_row(r), :]

                below = [get(c, px, start - 1) for c in range(2)]
                here = [get(c, px, start) for c in range(2)]
                for i in range(rows):
                    r = start + i
                    above = [get(c, px, r + 1) for c in range(2)]
                    re, im = [
                        (get(c, px - 1, r) + get(c, px + 1, r))
                        + (below[c] + above[c])
                        + side[i * 32 + c * COLS : i * 32 + c * COLS + COLS]
                        for c in range(2)
                    ]
                    re = re + src[px, at_row(r), :]
                    p, q = spread(gre, px, r), spread(gim, px, r)
                    emit(px, r, (p * re - q * im, p * im + q * re))
                    below, here = here, above

        @pl.when(lax.rem(count, 2) == 1)
        def _():
            begin(even)

        @pl.when(lax.rem(count, 2) == 0)
        def _():
            begin(odd)

        def into(new):
            def emit(px, r, values):
                for c, v in enumerate(values):
                    new[c, px, at_row(r), :] = v

            return emit

        for level in range(DEPTH - 1, 0, -1):

            @pl.when(level <= count - 2)
            def _(level=level):
                old, new = (odd, even) if level % 2 == 0 else (even, odd)
                sweep(old, into(new), range(DEPTH, DEPTH + PLANES), level)
                for d in range(1, level + 1):
                    sweep(old, into(new), (DEPTH - d, DEPTH + PLANES - 1 + d), level - d)

        leave = leaving(node)

        @pl.when(node > 0)
        def _():
            for c in leave:
                c.wait()

        def finish(px, r, values):
            at = pl.ds(((px - DEPTH) * ROWS + r - DEPTH) * LANES, LANES)
            for c, v in enumerate(values):
                hi, lo = halves(v)
                cat[pl.ds(32 + c * COLS, COLS), at] = hi
                cat[pl.ds(c * COLS, COLS), at] = lo

        sweep(odd, finish, range(DEPTH, DEPTH + PLANES), 0)
        for c in leave:
            c.start()
        o = lax.dot_general(
            cat[32:96, :], cat[0:64, :], (((1,), (1,)), ((), ())), preferred_element_type=F32
        )
        o = jnp.concatenate([o, jnp.zeros((64, 64), F32)], 1)
        lane = lax.broadcasted_iota(jnp.int32, (COLS, LANES), 1)
        seen = o[32:48] + o[48:64]
        proj = seen + pltpu.roll(seen, LANES - 32, 1)
        proj = pltpu.roll(jnp.where(lane < 32, proj, 0.0), 32 * lax.rem(node, 4), 1)
        part_ref[pl.ds(pl.multiple_of(16 * (node // 4), 16), 16), :] += proj
        half = o[0:32] + 0.5 * pltpu.roll(o[0:32], LANES - 32, 1)
        gram = half[0:16] + pltpu.roll(half[16:32], LANES - 16, 1)
        gram = jnp.where(lane < 16, gram, 0.0)
        part_ref[32:48, :] += pltpu.roll(gram, 16 * node, 1)

    for c in leaving(0):
        c.wait()


def solve(at, freqs, counts, own, pair, cross, even, odd, probe):
    cells = PLANES * ROWS * LANES
    return pl.pallas_call(
        solve_kernel,
        out_shape=(
            jax.ShapeDtypeStruct((QUAD * 64, cells), BF16),
            jax.ShapeDtypeStruct((48, LANES), F32),
        ),
        in_specs=[SMEM, SMEM, SMEM] + [ANY] * 6,
        out_specs=(
            pl.BlockSpec(memory_space=pltpu.HBM),
            VMEM,
        ),
        scratch_shapes=[
            pltpu.VMEM((SPAN, WIDE * COLS, LANES), F32),
            pltpu.VMEM((2, SPAN, WIDE * COLS, LANES), F32),
            pltpu.VMEM((2, SPAN, WIDE * COLS, LANES), F32),
            pltpu.VMEM((2 * LANES, LANES), BF16),
            pltpu.VMEM((SPAN, 32, LANES), F32),
            pltpu.VMEM((SPAN, 32, LANES), F32),
            pltpu.VMEM((SPAN, 32, LANES), F32),
            pltpu.VMEM((96, cells), BF16),
            pltpu.VMEM((352, LANES), F32),
            pltpu.SemaphoreType.DMA((24,)),
            pltpu.SemaphoreType.DMA((8,)),
        ],
        compiler_params=pltpu.CompilerParams(vmem_limit_bytes=SOLVE_LIMIT),
        name="solve",
    )(at, freqs, counts, own, pair, cross, even, odd, probe)


def respond_kernel(pick_ref, weight_ref, sum_ref, full_ref, out_ref, gram_ref, coef, full, sems):
    parts = PLANES * ROWS // STEP
    wide = STEP * LANES
    copies = [
        [
            pltpu.make_async_copy(
                full_ref.at[pl.ds(128 * j, 128), pl.ds(t * wide, wide)],
                full.at[t, pl.ds(128 * j, 128), :],
                sems.at[t, j],
            )
            for j in range(4)
        ]
        for t in range(parts)
    ]
    for group in copies:
        for c in group:
            c.start()
    lane = lax.broadcasted_iota(jnp.int32, (16, LANES), 1)
    for half in range(2):
        scale = weight_ref[half * 4] * (1.0 / QUAD)
        for j in range(1, 4):
            scale = jnp.where(lane < 32 * j, scale, weight_ref[half * 4 + j] * (1.0 / QUAD))
        acc = sum_ref[16 * half : 16 * half + 16, :] * scale
        for b in range(2):
            one = pltpu.roll(acc, 64, 1) if b else acc
            twice = jnp.where(
                lane < 32,
                one,
                jnp.where(lane < 96, pltpu.roll(one, 32, 1), pltpu.roll(one, 64, 1)),
            )
            at = pl.ds((half * 2 + b) * LANES, LANES)
            hi = twice.astype(BF16)
            coef[0:16, at] = hi
            coef[16:32, at] = (twice - hi.astype(F32)).astype(BF16)
    node = pick_ref[0]
    gram = pltpu.roll(sum_ref[32:48, :], lax.rem(128 - 16 * node, 128), 1)
    gram = gram * (weight_ref[node] * (1.0 / CELLS))
    gram_ref[:, 0:16] = gram[:, 0:16] + gram.T[0:16, :]

    flat = out_ref.reshape(16 * PLANES * ROWS, LANES)
    for t, group in enumerate(copies):
        for c in group:
            c.wait()
        big = jnp.dot(coef[...], full[t], preferred_element_type=F32)
        res = big[0:16] + big[16:32]
        for y in range(STEP):
            flat[pl.ds(t * STEP + y, 16, stride=PLANES * ROWS), :] = res[
                :, y * LANES : (y + 1) * LANES
            ]


def respond(pick, weights, total, full):
    parts = PLANES * ROWS // STEP
    return pl.pallas_call(
        respond_kernel,
        out_shape=(
            jax.ShapeDtypeStruct((16, PLANES, ROWS, LANES), F32),
            jax.ShapeDtypeStruct((16, LANES), F32),
        ),
        in_specs=[SMEM, SMEM, VMEM, ANY],
        out_specs=(VMEM, VMEM),
        scratch_shapes=[
            pltpu.VMEM((32, QUAD * 64), BF16),
            pltpu.VMEM((parts, QUAD * 64, STEP * LANES), BF16),
            pltpu.SemaphoreType.DMA((parts, 4)),
        ],
        compiler_params=pltpu.CompilerParams(vmem_limit_bytes=50 << 20),
        name="respond",
    )(pick, weights, total, full)


def both_ways(pairs):
    return pairs + [(b, a) for a, b in pairs]


def swap_core(v):
    return lax.ppermute(v, "row", [(r, r ^ 1) for r in range(16)])


def swap_rows(v, step, chosen):
    pairs = []
    for node in range(8):
        for r in range(16 - step):
            if chosen(r):
                other = node ^ 4 if (r // 2) % 2 else node
                pairs.append((node * 16 + r, other * 16 + r + step))
    return lax.ppermute(v, ("node", "row"), both_ways(pairs))


def xor_sum(x, axis, size, masks):
    combos = [0]
    for m in masks:
        combos += [c ^ m for c in combos]
    got = [x if c == 0 else lax.ppermute(x, axis, [(i, i ^ c) for i in range(size)]) for c in combos]
    while len(got) > 1:
        got = [got[i] + got[i + 1] for i in range(0, len(got), 2)]
    return got[0]


def turn(v, mask):
    return lax.ppermute(v, "node", [(i, i ^ mask) for i in range(8)])


def across(v):
    return lax.ppermute(v, "node", [(i, i ^ 4) for i in range(8)])


def place_into(out_ref, spot_ref, pieces, spots, sems):
    copies = []
    for piece, (slot, first) in zip(pieces, spots):
        at = pl.multiple_of(spot_ref[slot], ROWS)
        for i in range(0, piece.shape[0], 4):
            dst = out_ref.at[pl.ds(first + i, 4), :, pl.ds(at, ROWS), :]
            copies.append(pltpu.make_async_copy(piece.at[pl.ds(i, 4)], dst, sems.at[len(copies)]))
    for c in copies:
        c.start()
    for c in copies:
        c.wait()


EARLY = ((0, 0), (1, 0), (2, 0), (4, 0), (3, 0), (3, 8))
LATE = ((5, 0), (6, 0), (7, 0), (7, 8))


def early_kernel(spot_ref, *refs):
    place_into(refs[6], spot_ref, refs[:6], EARLY, refs[7])


def late_kernel(spot_ref, *refs):
    place_into(refs[5], spot_ref, refs[:4], LATE, refs[6])


def place(spots, early, late):
    whole = jax.ShapeDtypeStruct((16, PLANES, 128, LANES), F32)
    params = pltpu.CompilerParams(vmem_limit_bytes=50 << 20)
    begun = pl.pallas_call(
        early_kernel,
        out_shape=whole,
        in_specs=[SMEM] + [VMEM] * 6,
        out_specs=ANY,
        scratch_shapes=[pltpu.SemaphoreType.DMA((20,))],
        compiler_params=params,
        name="early",
    )(spots, *early)
    return pl.pallas_call(
        late_kernel,
        out_shape=whole,
        in_specs=[SMEM] + [VMEM] * 4 + [ANY],
        out_specs=ANY,
        scratch_shapes=[pltpu.SemaphoreType.DMA((12,))],
        input_output_aliases={5: 0},
        compiler_params=params,
        name="late",
    )(spots, *late, begun)


def local(inputs, diagonal, observations, frequencies, weights, counts, assignment):
    node = lax.axis_index("node")
    row = lax.axis_index("row")
    core, odd = row % 2, (row // 2) % 2
    other = jnp.where(core == odd, node ^ 4, node)
    at = jnp.stack([16 * node, 16 * other, core, odd]).astype(jnp.int32)
    s1, s2, s3, s4 = pack(at, inputs, diagonal)
    own, probe = prep(at, inputs, diagonal, observations, s3)
    cross = swap_rows(s2, 1, lambda r: r % 2 == 1)
    far_even = swap_rows(s3, 2, lambda r: (r // 2) % 2 == 0)
    far_odd = swap_rows(s4, 2, lambda r: (r // 2) % 2 == 1)
    pair = swap_core(s1)
    fields, part = solve(at, frequencies, counts, own, pair, cross, far_even, far_odd, probe)
    total = xor_sum(part, "row", 16, [1, 2])
    total = xor_sum(total, "row", 16, [4, 8])
    total = xor_sum(total, "node", 8, [1, 2])
    total = xor_sum(total, "node", 8, [4])
    pick = lax.dynamic_slice_in_dim(assignment, node, 1)
    mine, gram = respond(pick, weights, total, fields)

    left, right, other = turn(mine, 1), turn(mine, 3), across(mine)
    far0, far1 = turn(right[:8], 1), turn(left[8:], 3)
    left_o, right_o = turn(other, 1), turn(other, 3)
    far0_o, far1_o = across(far0), across(far1)
    x, z = node % 4, node // 4
    spots = []
    for side in (z, 1 - z):
        spots += [(side * 4 + (x ^ mask)) * ROWS for mask in (0, 1, 3, 2)]
    full = place(
        jnp.stack(spots).astype(jnp.int32),
        (mine, left, right, other, far0, far1),
        (left_o, right_o, far0_o, far1_o),
    )
    return full, gram[None, :, :16]


def solution(mesh):
    placed = (
        P(None, "row", None, None),
        P("row", None, None),
        P(None, "row", None, None),
        P(),
        P(),
        P(),
        P(),
    )
    return jax.shard_map(
        local,
        mesh=mesh,
        in_specs=placed,
        out_specs=(P(None, "row", None, None), P("node", None, None)),
        check_vma=False,
    )
```

profile of v0, /device:TPU:6, one launch (start us, length us, event | category | flops | bytes accessed | tf_op | source)
XLA Modules:
  0.0 135.1 jit_solution(9699920396523427309)
XLA Ops:
  0.7 0.1 pad_add_fusion.at_ref
  0.7 0.0 copy-start
  0.7 0.9 copy-done
  1.7 4.1 %pack.1 = (f32[1440,128]{1,0:T(8,128)S(1)}, f32[1440,128]{1,0:T(8,128)S(1)}, f32[272,128]{1,0:T(8,128)S(1)}, f32[272,128]{1,0:T(8,128)S(1)}) custom-call(s32[4]{0:T(128)S(1)} %pad_add_fusion.at_ref, f32[16,4,128,128]{3,2,1,0:T(8,128)} %src_ref.3, f32[4,128,128]{2,1,0:T(8,128)S(1)} %copy-done), custom_call_target="tpu_custom_call" | custom-call | tf_op jit(solution)/shard_map/pack/pallas_call | solution.py:102
  5.8 0.1 collective-permute-start
  5.9 0.7 collective-permute-start.1
  6.6 3.4 %collective-permute-start.2 = (f32[272,128]{1,0:T(8,128)S(1)}, f32[272,128]{1,0:T(8,128)S(1)}, u32[]{:S(2)}, u32[]{:S(2)}) collective-permute-start(f32[272,128]{1,0:T(8,128)S(1)} %get-tuple-element.12.after_ref), channel_id=1, source_target_pairs={{0,2},{1,3},{4,6},{5,7},{8,10},{9,11},{12,14},{13,15},{16,18},{17,... | collective-permute-start | bytes 417800 | tf_op jit(solution)/shard_map/ppermute | solution.py:491
  10.0 0.8 collective-permute-start.3
  10.8 3.3 %prep.1 = (f32[1792,128]{1,0:T(8,128)S(1)}, bf16[32,8192]{1,0:T(8,128)(2,1)S(1)}) custom-call(s32[4]{0:T(128)S(1)} %pad_add_fusion.at_ref, f32[16,4,128,128]{3,2,1,0:T(8,128)} %src_ref.3, f32[4,128,128]{2,1,0:T(8,128)S(1)} %copy-done, f32[16,4,128,128]{3,2,1,0:T(8,128)} %obs_ref.1, f32[272,128]{1,0:T(8,128)S(1)} %get-tuple-element.12.after_ref), custom_call_target="tpu_custom_call" | custom-call | flops 40000000 | bytes 4000000 | tf_op jit(solution)/shard_map/prep/pallas_call | solution.py:151
  14.1 0.0 copy-start.1
  14.1 0.9 copy-done.1
  15.0 7.3 %collective-permute-done.2.even_ref = f32[272,128]{1,0:T(8,128)S(1)} collective-permute-done((f32[272,128]{1,0:T(8,128)S(1)}, f32[272,128]{1,0:T(8,128)S(1)}, u32[]{:S(2)}, u32[]{:S(2)}) %collective-permute-start.2) | collective-permute-done | bytes 139296 | tf_op jit(solution)/shard_map/ppermute | solution.py:491
  22.3 0.0 collective-permute-done.3.odd_ref
  22.3 0.0 collective-permute-done.pair_ref
  22.3 0.0 collective-permute-done.1.cross_ref
  22.3 0.0 copy-done.2
  22.3 0.0 copy-done.3
  22.3 42.9 %solve.1 = (bf16[512,8192]{1,0:T(8,128)(2,1)}, f32[48,128]{1,0:T(8,128)S(1)}) custom-call(s32[4]{0:T(128)S(1)} %pad_add_fusion.at_ref, f32[8]{0:T(128)S(1)} %copy-done.2, s32[8]{0:T(128)S(1)} %copy-done.3, f32[1792,128]{1,0:T(8,128)} %copy-done.1, f32[1440,128]{1,0:T(8,128)S(1)} %collective-permute-done.pair_ref, ...), custom_call_target="tpu_custom_call" | custom-call | tf_op jit(solution)/shard_map/solve/pallas_call | solution.py:376
  65.3 0.1 collective-permute-start.4
  65.4 2.9 %collective-permute-start.5 = (f32[48,128]{1,0:T(8,128)S(1)}, f32[48,128]{1,0:T(8,128)S(1)}, u32[]{:S(2)}, u32[]{:S(2)}) collective-permute-start(f32[48,128]{1,0:T(8,128)S(1)} %get-tuple-element.18), channel_id=1, source_target_pairs={{0,2},{1,3},{2,0},{3,1},{4,6},{5,7},{6,4},{7,5},{8,10},{9,11},{10,... | collective-permute-start | bytes 73736 | tf_op jit(solution)/shard_map/ppermute | solution.py:498
  68.2 0.0 collective-permute-start.6
  68.3 0.0 collective-permute-done.4
  68.3 1.8 %collective-permute-done.5 = f32[48,128]{1,0:T(8,128)S(1)} collective-permute-done((f32[48,128]{1,0:T(8,128)S(1)}, f32[48,128]{1,0:T(8,128)S(1)}, u32[]{:S(2)}, u32[]{:S(2)}) %collective-permute-start.5) | collective-permute-done | bytes 24608 | tf_op jit(solution)/shard_map/ppermute | solution.py:498
  70.1 1.4 %collective-permute-done.6 = f32[48,128]{1,0:T(8,128)S(1)} collective-permute-done((f32[48,128]{1,0:T(8,128)S(1)}, f32[48,128]{1,0:T(8,128)S(1)}, u32[]{:S(2)}, u32[]{:S(2)}) %collective-permute-start.6) | collective-permute-done | bytes 24608 | tf_op jit(solution)/shard_map/ppermute | solution.py:498
  71.5 1.8 %collective-permute-start.7 = (f32[48,128]{1,0:T(8,128)S(1)}, f32[48,128]{1,0:T(8,128)S(1)}, u32[]{:S(2)}, u32[]{:S(2)}) collective-permute-start(f32[48,128]{1,0:T(8,128)S(1)} %add_add_fusion.2), channel_id=1, source_target_pairs={{0,4},{1,5},{2,6},{3,7},{4,0},{5,1},{6,2},{7,3},{8,12},{9,13},{10,... | collective-permute-start | bytes 73736 | tf_op jit(solution)/shard_map/ppermute | solution.py:498
  73.3 2.4 %collective-permute-start.8 = (f32[48,128]{1,0:T(8,128)S(1)}, f32[48,128]{1,0:T(8,128)S(1)}, u32[]{:S(2)}, u32[]{:S(2)}) collective-permute-start(f32[48,128]{1,0:T(8,128)S(1)} %add_add_fusion.2), channel_id=1, source_target_pairs={{0,8},{1,9},{2,10},{3,11},{4,12},{5,13},{6,14},{7,15},{8,0},{9,1},... | collective-permute-start | bytes 73736 | tf_op jit(solution)/shard_map/ppermute | solution.py:498
  75.8 0.7 collective-permute-start.9
  76.5 0.0 collective-permute-done.7
  76.5 2.2 %collective-permute-done.8 = f32[48,128]{1,0:T(8,128)S(1)} collective-permute-done((f32[48,128]{1,0:T(8,128)S(1)}, f32[48,128]{1,0:T(8,128)S(1)}, u32[]{:S(2)}, u32[]{:S(2)}) %collective-permute-start.8) | collective-permute-done | bytes 24608 | tf_op jit(solution)/shard_map/ppermute | solution.py:498
  78.7 2.1 %collective-permute-done.9 = f32[48,128]{1,0:T(8,128)S(1)} collective-permute-done((f32[48,128]{1,0:T(8,128)S(1)}, f32[48,128]{1,0:T(8,128)S(1)}, u32[]{:S(2)}, u32[]{:S(2)}) %collective-permute-start.9) | collective-permute-done | bytes 24608 | tf_op jit(solution)/shard_map/ppermute | solution.py:498
  80.8 0.9 collective-permute-start.10
  81.7 1.1 collective-permute-start.11
  82.8 2.8 %collective-permute-start.12 = (f32[48,128]{1,0:T(8,128)S(1)}, f32[48,128]{1,0:T(8,128)S(1)}, u32[]{:S(2)}, u32[]{:S(2)}) collective-permute-start(f32[48,128]{1,0:T(8,128)S(1)} %add_add_fusion.1), channel_id=1, source_target_pairs={{0,48},{16,32},{32,16},{48,0},{64,112},{80,96},{96,80},{112,64},{1... | collective-permute-start | bytes 73736 | tf_op jit(solution)/shard_map/ppermute | solution.py:498
  85.6 0.0 collective-permute-done.10
  85.6 1.5 %collective-permute-done.11 = f32[48,128]{1,0:T(8,128)S(1)} collective-permute-done((f32[48,128]{1,0:T(8,128)S(1)}, f32[48,128]{1,0:T(8,128)S(1)}, u32[]{:S(2)}, u32[]{:S(2)}) %collective-permute-start.11) | collective-permute-done | bytes 24608 | tf_op jit(solution)/shard_map/ppermute | solution.py:498
  87.0 0.8 collective-permute-done.12
  87.9 4.2 %collective-permute-start.13 = (f32[48,128]{1,0:T(8,128)S(1)}, f32[48,128]{1,0:T(8,128)S(1)}, u32[]{:S(2)}, u32[]{:S(2)}) collective-permute-start(f32[48,128]{1,0:T(8,128)S(1)} %add_add_fusion), channel_id=1, source_target_pairs={{0,64},{16,80},{32,96},{48,112},{64,0},{80,16},{96,32},{112,48},{1... | collective-permute-start | bytes 73736 | tf_op jit(solution)/shard_map/ppermute | solution.py:498
  92.1 0.0 copy-done.5
  92.1 0.6 dynamic_slice.3.pick_ref
  92.6 1.2 collective-permute-done.13
  93.9 0.0 copy-done.4
  93.9 5.2 %respond.1 = (f32[16,4,16,128]{3,2,1,0:T(8,128)S(1)}, f32[16,128]{1,0:T(8,128)S(1)}) custom-call(s32[1]{0:T(128)} %dynamic_slice.3.pick_ref, f32[8]{0:T(128)S(1)} %copy-done.4, f32[48,128]{1,0:T(8,128)S(1)} %add.90.sum_ref, bf16[512,8192]{1,0:T(8,128)(2,1)} %get-tuple-element.19.full_ref), custom_call_target="tpu_custom_call" | custom-call | tf_op jit(solution)/shard_map/respond/pallas_call | solution.py:458
  99.1 2.8 %collective-permute-start.17 = (f32[16,4,16,128]{3,2,1,0:T(8,128)S(1)}, f32[16,4,16,128]{3,2,1,0:T(8,128)S(1)}, u32[]{:S(2)}, u32[]{:S(2)}) collective-permute-start(f32[16,4,16,128]{3,2,1,0:T(8,128)S(1)} %get-tuple-element.20.refs_0_), channel_id=1, source_target_pairs={{0,48},{16,32},{32,16},{48,0},{64,112},{80,96},{96,80},{112,64},{1... | collective-permute-start | bytes 1572872 | tf_op jit(solution)/shard_map/ppermute | solution.py:505
  101.9 0.0 collective-permute-start.20
  101.9 3.5 %collective-permute-start.14 = (f32[16,4,16,128]{3,2,1,0:T(8,128)S(1)}, f32[16,4,16,128]{3,2,1,0:T(8,128)S(1)}, u32[]{:S(2)}, u32[]{:S(2)}) collective-permute-start(f32[16,4,16,128]{3,2,1,0:T(8,128)S(1)} %get-tuple-element.20.refs_0_), channel_id=1, source_target_pairs={{0,64},{16,80},{32,96},{48,112},{64,0},{80,16},{96,32},{112,48},{1... | collective-permute-start | bytes 1572872 | tf_op jit(solution)/shard_map/ppermute | solution.py:509
  105.4 5.0 %collective-permute-done.17.refs_2_ = f32[16,4,16,128]{3,2,1,0:T(8,128)S(1)} collective-permute-done((f32[16,4,16,128]{3,2,1,0:T(8,128)S(1)}, f32[16,4,16,128]{3,2,1,0:T(8,128)S(1)}, u32[]{:S(2)}, u32[]{:S(2)}) %collective-permute-start.17) | collective-permute-done | bytes 524320 | tf_op jit(solution)/shard_map/ppermute | solution.py:505
  110.4 0.1 collective-permute-start.18
  110.5 4.7 %collective-permute-done.20.refs_1_ = f32[16,4,16,128]{3,2,1,0:T(8,128)S(1)} collective-permute-done((f32[16,4,16,128]{3,2,1,0:T(8,128)S(1)}, f32[16,4,16,128]{3,2,1,0:T(8,128)S(1)}, u32[]{:S(2)}, u32[]{:S(2)}) %collective-permute-start.20) | collective-permute-done | bytes 524320 | tf_op jit(solution)/shard_map/ppermute | solution.py:505
  115.3 0.1 collective-permute-start.21
  115.4 0.0 collective-permute-done.14.refs_3_
  115.4 0.4 collective-permute-start.15
  115.8 2.9 %collective-permute-start.16 = (f32[16,4,16,128]{3,2,1,0:T(8,128)S(1)}, f32[16,4,16,128]{3,2,1,0:T(8,128)S(1)}, u32[]{:S(2)}, u32[]{:S(2)}) collective-permute-start(f32[16,4,16,128]{3,2,1,0:T(8,128)S(1)} %collective-permute-done.14.refs_3_), channel_id=1, source_target_pairs={{0,48},{16,32},{32,16},{48,0},{64,112},{80,96},{96,80},{112,64},{1... | collective-permute-start | bytes 1572872 | tf_op jit(solution)/shard_map/ppermute | solution.py:505
  118.6 2.3 %collective-permute-done.18.refs_4_ = f32[8,4,16,128]{3,2,1,0:T(8,128)S(1)} collective-permute-done((f32[8,4,16,128]{3,2,1,0:T(8,128)S(1)}, f32[8,4,16,128]{3,2,1,0:T(8,128)S(1)}, u32[]{:S(2)}, u32[]{:S(2)}) %collective-permute-start.18) | collective-permute-done | bytes 262176 | tf_op jit(solution)/shard_map/ppermute | solution.py:505
  120.9 3.5 %collective-permute-start.19 = (f32[8,4,16,128]{3,2,1,0:T(8,128)S(1)}, f32[8,4,16,128]{3,2,1,0:T(8,128)}, u32[]{:S(2)}, u32[]{:S(2)}) collective-permute-start(f32[8,4,16,128]{3,2,1,0:T(8,128)S(1)} %collective-permute-done.18.refs_4_), channel_id=1, source_target_pairs={{0,64},{16,80},{32,96},{48,112},{64,0},{80,16},{96,32},{112,48},{1... | collective-permute-start | bytes 786440 | tf_op jit(solution)/shard_map/ppermute | solution.py:509
  124.4 0.0 collective-permute-done.21.refs_5_
  124.4 2.2 %collective-permute-start.22 = (f32[8,4,16,128]{3,2,1,0:T(8,128)}, f32[8,4,16,128]{3,2,1,0:T(8,128)}, u32[]{:S(2)}, u32[]{:S(2)}) collective-permute-start(f32[8,4,16,128]{3,2,1,0:T(8,128)} %collective-permute-done.21.refs_5_), channel_id=1, source_target_pairs={{0,64},{16,80},{32,96},{48,112},{64,0},{80,16},{96,32},{112,48},{1... | collective-permute-start | bytes 786440 | tf_op jit(solution)/shard_map/ppermute | solution.py:509
  126.6 0.1 stack.50.spot_ref
  126.7 0.6 slice_bitcast_fusion
  127.3 2.6 %early.1.refs_4_ = f32[16,4,128,128]{3,2,1,0:T(8,128)} custom-call(s32[8]{0:T(128)S(1)} %stack.50.spot_ref, f32[16,4,16,128]{3,2,1,0:T(8,128)S(1)} %get-tuple-element.20.refs_0_, f32[16,4,16,128]{3,2,1,0:T(8,128)S(1)} %collective-permute-done.20.refs_1_, f32[16,4,16,128]{3,2,1,0:T(8,128)S(1)} %collective-permute-done.17.refs_2_, ...), custom_call_target="tpu_custom_call" | custom-call | tf_op jit(solution)/shard_map/early/pallas_call | solution.py:540
  129.9 0.0 collective-permute-done.19.refs_2_
  129.9 2.7 %collective-permute-done.22.refs_3_ = f32[8,4,16,128]{3,2,1,0:T(8,128)} collective-permute-done((f32[8,4,16,128]{3,2,1,0:T(8,128)}, f32[8,4,16,128]{3,2,1,0:T(8,128)}, u32[]{:S(2)}, u32[]{:S(2)}) %collective-permute-start.22) | collective-permute-done | bytes 262176 | tf_op jit(solution)/shard_map/ppermute | solution.py:509
  132.6 0.0 collective-permute-done.15.refs_0_
  132.6 0.0 collective-permute-done.16.refs_1_
  132.6 2.3 %late.1 = f32[16,4,128,128]{3,2,1,0:T(8,128)} custom-call(s32[8]{0:T(128)S(1)} %stack.50.spot_ref, f32[16,4,16,128]{3,2,1,0:T(8,128)S(1)} %collective-permute-done.15.refs_0_, f32[16,4,16,128]{3,2,1,0:T(8,128)S(1)} %collective-permute-done.16.refs_1_, f32[8,4,16,128]{3,2,1,0:T(8,128)} %collective-permute-done.19.refs_2_, ...), custom_call_target="tpu_custom_call", output_to_operand_aliasing={{}: (5, {})} | custom-call | tf_op jit(solution)/shard_map/late/pallas_call | solution.py:549
  (10 shorter events, 0.1 us)
Async XLA Ops:
  0.7 1.0 copy-start
  5.8 16.5 %collective-permute-start = (f32[1440,128]{1,0:T(8,128)S(1)}, f32[1440,128]{1,0:T(8,128)S(1)}, u32[]{:S(2)}, u32[]{:S(2)}) collective-permute-start(f32[1440,128]{1,0:T(8,128)S(1)} %get-tuple-element.14), channel_id=1, source_target_pairs={{0,1},{1,0},{2,3},{3,2},{4,5},{5,4},{6,7},{7,6},{8,9},{9,8},{10,11... | collective-permute-start | bytes 2211848 | tf_op jit(solution)/shard_map/ppermute | solution.py:481
  5.9 16.4 %collective-permute-start.1 = (f32[1440,128]{1,0:T(8,128)S(1)}, f32[1440,128]{1,0:T(8,128)S(1)}, u32[]{:S(2)}, u32[]{:S(2)}) collective-permute-start(f32[1440,128]{1,0:T(8,128)S(1)} %get-tuple-element.15), channel_id=1, source_target_pairs={{1,2},{3,68},{5,6},{7,72},{9,10},{11,76},{13,14},{17,18},{19,84},{... | collective-permute-start | bytes 2211848 | tf_op jit(solution)/shard_map/ppermute | solution.py:491
  6.6 15.7 %collective-permute-start.2 = (f32[272,128]{1,0:T(8,128)S(1)}, f32[272,128]{1,0:T(8,128)S(1)}, u32[]{:S(2)}, u32[]{:S(2)}) collective-permute-start(f32[272,128]{1,0:T(8,128)S(1)} %get-tuple-element.12.after_ref), channel_id=1, source_target_pairs={{0,2},{1,3},{4,6},{5,7},{8,10},{9,11},{12,14},{13,15},{16,18},{17,... | collective-permute-start | bytes 417800 | tf_op jit(solution)/shard_map/ppermute | solution.py:491
  10.0 12.3 %copy-start.2 = (f32[8]{0:T(128)S(1)}, f32[8]{0:T(128)}, u32[]{:S(2)}) copy-start(f32[8]{0:T(128)} %freq_ref.1) | copy-start | bytes 100
  10.0 12.3 %copy-start.3 = (s32[8]{0:T(128)S(1)}, s32[8]{0:T(128)}, u32[]{:S(2)}) copy-start(s32[8]{0:T(128)} %count_ref.1) | copy-start | bytes 100
  10.0 82.1 %copy-start.5 = (s32[8]{0:T(128)S(1)}, s32[8]{0:T(128)}, u32[]{:S(2)}) copy-start(s32[8]{0:T(128)} %param.13) | copy-start | bytes 100
  10.0 83.9 %copy-start.4 = (f32[8]{0:T(128)S(1)}, f32[8]{0:T(128)}, u32[]{:S(2)}) copy-start(f32[8]{0:T(128)} %weight_ref.1) | copy-start | bytes 100
  10.0 12.3 %collective-permute-start.3 = (f32[272,128]{1,0:T(8,128)S(1)}, f32[272,128]{1,0:T(8,128)S(1)}, u32[]{:S(2)}, u32[]{:S(2)}) collective-permute-start(f32[272,128]{1,0:T(8,128)S(1)} %get-tuple-element.16), channel_id=1, source_target_pairs={{2,68},{3,69},{6,72},{7,73},{10,76},{11,77},{18,84},{19,85},{22,88... | collective-permute-start | bytes 417800 | tf_op jit(solution)/shard_map/ppermute | solution.py:491
  14.1 0.9 copy-start.1
  65.3 3.0 %collective-permute-start.4 = (f32[48,128]{1,0:T(8,128)S(1)}, f32[48,128]{1,0:T(8,128)S(1)}, u32[]{:S(2)}, u32[]{:S(2)}) collective-permute-start(f32[48,128]{1,0:T(8,128)S(1)} %get-tuple-element.18), channel_id=1, source_target_pairs={{0,1},{1,0},{2,3},{3,2},{4,5},{5,4},{6,7},{7,6},{8,9},{9,8},{10,11... | collective-permute-start | bytes 73736 | tf_op jit(solution)/shard_map/ppermute | solution.py:498
  65.4 4.7 %collective-permute-start.5 = (f32[48,128]{1,0:T(8,128)S(1)}, f32[48,128]{1,0:T(8,128)S(1)}, u32[]{:S(2)}, u32[]{:S(2)}) collective-permute-start(f32[48,128]{1,0:T(8,128)S(1)} %get-tuple-element.18), channel_id=1, source_target_pairs={{0,2},{1,3},{2,0},{3,1},{4,6},{5,7},{6,4},{7,5},{8,10},{9,11},{10,... | collective-permute-start | bytes 73736 | tf_op jit(solution)/shard_map/ppermute | solution.py:498
  68.2 3.3 %collective-permute-start.6 = (f32[48,128]{1,0:T(8,128)S(1)}, f32[48,128]{1,0:T(8,128)S(1)}, u32[]{:S(2)}, u32[]{:S(2)}) collective-permute-start(f32[48,128]{1,0:T(8,128)S(1)} %get-tuple-element.18), channel_id=1, source_target_pairs={{0,3},{1,2},{2,1},{3,0},{4,7},{5,6},{6,5},{7,4},{8,11},{9,10},{10,... | collective-permute-start | bytes 73736 | tf_op jit(solution)/shard_map/ppermute | solution.py:498
  71.5 5.0 %collective-permute-start.7 = (f32[48,128]{1,0:T(8,128)S(1)}, f32[48,128]{1,0:T(8,128)S(1)}, u32[]{:S(2)}, u32[]{:S(2)}) collective-permute-start(f32[48,128]{1,0:T(8,128)S(1)} %add_add_fusion.2), channel_id=1, source_target_pairs={{0,4},{1,5},{2,6},{3,7},{4,0},{5,1},{6,2},{7,3},{8,12},{9,13},{10,... | collective-permute-start | bytes 73736 | tf_op jit(solution)/shard_map/ppermute | solution.py:498
  73.3 5.3 %collective-permute-start.8 = (f32[48,128]{1,0:T(8,128)S(1)}, f32[48,128]{1,0:T(8,128)S(1)}, u32[]{:S(2)}, u32[]{:S(2)}) collective-permute-start(f32[48,128]{1,0:T(8,128)S(1)} %add_add_fusion.2), channel_id=1, source_target_pairs={{0,8},{1,9},{2,10},{3,11},{4,12},{5,13},{6,14},{7,15},{8,0},{9,1},... | collective-permute-start | bytes 73736 | tf_op jit(solution)/shard_map/ppermute | solution.py:498
  75.8 5.0 %collective-permute-start.9 = (f32[48,128]{1,0:T(8,128)S(1)}, f32[48,128]{1,0:T(8,128)S(1)}, u32[]{:S(2)}, u32[]{:S(2)}) collective-permute-start(f32[48,128]{1,0:T(8,128)S(1)} %add_add_fusion.2), channel_id=1, source_target_pairs={{0,12},{1,13},{2,14},{3,15},{4,8},{5,9},{6,10},{7,11},{8,4},{9,5},... | collective-permute-start | bytes 73736 | tf_op jit(solution)/shard_map/ppermute | solution.py:498
  80.8 4.8 %collective-permute-start.10 = (f32[48,128]{1,0:T(8,128)S(1)}, f32[48,128]{1,0:T(8,128)S(1)}, u32[]{:S(2)}, u32[]{:S(2)}) collective-permute-start(f32[48,128]{1,0:T(8,128)S(1)} %add_add_fusion.1), channel_id=1, source_target_pairs={{0,16},{16,0},{32,48},{48,32},{64,80},{80,64},{96,112},{112,96},{1... | collective-permute-start | bytes 73736 | tf_op jit(solution)/shard_map/ppermute | solution.py:498
  81.7 5.3 %collective-permute-start.11 = (f32[48,128]{1,0:T(8,128)S(1)}, f32[48,128]{1,0:T(8,128)S(1)}, u32[]{:S(2)}, u32[]{:S(2)}) collective-permute-start(f32[48,128]{1,0:T(8,128)S(1)} %add_add_fusion.1), channel_id=1, source_target_pairs={{0,32},{16,48},{32,0},{48,16},{64,96},{80,112},{96,64},{112,80},{1... | collective-permute-start | bytes 73736 | tf_op jit(solution)/shard_map/ppermute | solution.py:498
  82.8 5.0 %collective-permute-start.12 = (f32[48,128]{1,0:T(8,128)S(1)}, f32[48,128]{1,0:T(8,128)S(1)}, u32[]{:S(2)}, u32[]{:S(2)}) collective-permute-start(f32[48,128]{1,0:T(8,128)S(1)} %add_add_fusion.1), channel_id=1, source_target_pairs={{0,48},{16,32},{32,16},{48,0},{64,112},{80,96},{96,80},{112,64},{1... | collective-permute-start | bytes 73736 | tf_op jit(solution)/shard_map/ppermute | solution.py:498
  87.9 6.0 %collective-permute-start.13 = (f32[48,128]{1,0:T(8,128)S(1)}, f32[48,128]{1,0:T(8,128)S(1)}, u32[]{:S(2)}, u32[]{:S(2)}) collective-permute-start(f32[48,128]{1,0:T(8,128)S(1)} %add_add_fusion), channel_id=1, source_target_pairs={{0,64},{16,80},{32,96},{48,112},{64,0},{80,16},{96,32},{112,48},{1... | collective-permute-start | bytes 73736 | tf_op jit(solution)/shard_map/ppermute | solution.py:498
  99.1 11.4 %collective-permute-start.17 = (f32[16,4,16,128]{3,2,1,0:T(8,128)S(1)}, f32[16,4,16,128]{3,2,1,0:T(8,128)S(1)}, u32[]{:S(2)}, u32[]{:S(2)}) collective-permute-start(f32[16,4,16,128]{3,2,1,0:T(8,128)S(1)} %get-tuple-element.20.refs_0_), channel_id=1, source_target_pairs={{0,48},{16,32},{32,16},{48,0},{64,112},{80,96},{96,80},{112,64},{1... | collective-permute-start | bytes 1572872 | tf_op jit(solution)/shard_map/ppermute | solution.py:505
  101.9 13.4 %collective-permute-start.20 = (f32[16,4,16,128]{3,2,1,0:T(8,128)S(1)}, f32[16,4,16,128]{3,2,1,0:T(8,128)S(1)}, u32[]{:S(2)}, u32[]{:S(2)}) collective-permute-start(f32[16,4,16,128]{3,2,1,0:T(8,128)S(1)} %get-tuple-element.20.refs_0_), channel_id=1, source_target_pairs={{0,16},{16,0},{32,48},{48,32},{64,80},{80,64},{96,112},{112,96},{1... | collective-permute-start | bytes 1572872 | tf_op jit(solution)/shard_map/ppermute | solution.py:505
  101.9 13.5 %collective-permute-start.14 = (f32[16,4,16,128]{3,2,1,0:T(8,128)S(1)}, f32[16,4,16,128]{3,2,1,0:T(8,128)S(1)}, u32[]{:S(2)}, u32[]{:S(2)}) collective-permute-start(f32[16,4,16,128]{3,2,1,0:T(8,128)S(1)} %get-tuple-element.20.refs_0_), channel_id=1, source_target_pairs={{0,64},{16,80},{32,96},{48,112},{64,0},{80,16},{96,32},{112,48},{1... | collective-permute-start | bytes 1572872 | tf_op jit(solution)/shard_map/ppermute | solution.py:509
  110.4 10.4 %collective-permute-start.18 = (f32[8,4,16,128]{3,2,1,0:T(8,128)S(1)}, f32[8,4,16,128]{3,2,1,0:T(8,128)S(1)}, u32[]{:S(2)}, u32[]{:S(2)}) collective-permute-start(f32[8,4,16,128]{3,2,1,0:T(8,128)S(1)} %slice.12), channel_id=1, source_target_pairs={{0,16},{16,0},{32,48},{48,32},{64,80},{80,64},{96,112},{112,96},{1... | collective-permute-start | bytes 786440 | tf_op jit(solution)/shard_map/ppermute | solution.py:505
  115.3 9.1 %collective-permute-start.21 = (f32[8,4,16,128]{3,2,1,0:T(8,128)S(1)}, f32[8,4,16,128]{3,2,1,0:T(8,128)}, u32[]{:S(2)}, u32[]{:S(2)}) collective-permute-start(f32[8,4,16,128]{3,2,1,0:T(8,128)S(1)} %slice.13), channel_id=1, source_target_pairs={{0,48},{16,32},{32,16},{48,0},{64,112},{80,96},{96,80},{112,64},{1... | collective-permute-start | bytes 786440 | tf_op jit(solution)/shard_map/ppermute | solution.py:505
  115.4 17.2 %collective-permute-start.15 = (f32[16,4,16,128]{3,2,1,0:T(8,128)S(1)}, f32[16,4,16,128]{3,2,1,0:T(8,128)S(1)}, u32[]{:S(2)}, u32[]{:S(2)}) collective-permute-start(f32[16,4,16,128]{3,2,1,0:T(8,128)S(1)} %collective-permute-done.14.refs_3_), channel_id=1, source_target_pairs={{0,16},{16,0},{32,48},{48,32},{64,80},{80,64},{96,112},{112,96},{1... | collective-permute-start | bytes 1572872 | tf_op jit(solution)/shard_map/ppermute | solution.py:505
  115.8 16.9 %collective-permute-start.16 = (f32[16,4,16,128]{3,2,1,0:T(8,128)S(1)}, f32[16,4,16,128]{3,2,1,0:T(8,128)S(1)}, u32[]{:S(2)}, u32[]{:S(2)}) collective-permute-start(f32[16,4,16,128]{3,2,1,0:T(8,128)S(1)} %collective-permute-done.14.refs_3_), channel_id=1, source_target_pairs={{0,48},{16,32},{32,16},{48,0},{64,112},{80,96},{96,80},{112,64},{1... | collective-permute-start | bytes 1572872 | tf_op jit(solution)/shard_map/ppermute | solution.py:505
  120.9 9.0 %collective-permute-start.19 = (f32[8,4,16,128]{3,2,1,0:T(8,128)S(1)}, f32[8,4,16,128]{3,2,1,0:T(8,128)}, u32[]{:S(2)}, u32[]{:S(2)}) collective-permute-start(f32[8,4,16,128]{3,2,1,0:T(8,128)S(1)} %collective-permute-done.18.refs_4_), channel_id=1, source_target_pairs={{0,64},{16,80},{32,96},{48,112},{64,0},{80,16},{96,32},{112,48},{1... | collective-permute-start | bytes 786440 | tf_op jit(solution)/shard_map/ppermute | solution.py:509
  124.4 8.2 %collective-permute-start.22 = (f32[8,4,16,128]{3,2,1,0:T(8,128)}, f32[8,4,16,128]{3,2,1,0:T(8,128)}, u32[]{:S(2)}, u32[]{:S(2)}) collective-permute-start(f32[8,4,16,128]{3,2,1,0:T(8,128)} %collective-permute-done.21.refs_5_), channel_id=1, source_target_pairs={{0,64},{16,80},{32,96},{48,112},{64,0},{80,16},{96,32},{112,48},{1... | collective-permute-start | bytes 786440 | tf_op jit(solution)/shard_map/ppermute | solution.py:509
where the time goes:
time: 138 us; the launch traced here: 135 us
  Pallas kernels  60.3 us (44%)
  starting transfers between devices  37.4 us (27%)
  waiting for transfers between devices  33.1 us (24%)
  local copies, waits for them, and re-layouts  3.19 us (2%)
    pallas_call x1, Pallas kernels, solve(): pl.pallas_call(solve_kernel, out_shape=(jax.ShapeDtypeStruct((QUAD * 64,...  42.9 us
    ppermute x10, starting transfers between devices, xor_sum(): lax.ppermute(x, axis, [(i, i ^ c) for i in range(size)])  16.9 us
    ppermute x6, waiting for transfers between devices, turn(): return lax.ppermute(v, 'node', [(i, i ^ mask) for i in range(8)])  12 us
    ppermute x10, waiting for transfers between devices, xor_sum(): lax.ppermute(x, axis, [(i, i ^ c) for i in range(size)])  11 us
    ppermute x3, starting transfers between devices, across(): return lax.ppermute(v, 'node', [(i, i ^ 4) for i in range(8)])  9.22 us
    ppermute x3, waiting for transfers between devices, swap_rows(): return lax.ppermute(v, ('node', 'row'), both_ways(pairs))  7.3 us
    ppermute x6, starting transfers between devices, turn(): return lax.ppermute(v, 'node', [(i, i ^ mask) for i in range(8)])  6.23 us
    pallas_call x1, Pallas kernels, respond(): pl.pallas_call(respond_kernel, out_shape=(jax.ShapeDtypeStruct((16, PLANE...  5.19 us
  transfers between devices with their start and end apart: 23, of which 12 were waited for; matrix products, arithmetic and copies ran while one was open for 1% of the time, Pallas kernels for 4%

commit v1 on v0

--- a/solution.py
+++ b/solution.py
@@ -19,7 +19,6 @@
 FAR_B = ROWS * COLS
 OWN_B = PLANES * WIDE * COLS
 STEP = 8
-PART = 2048
 PACK_LIMIT = 50 << 20
 SOLVE_LIMIT = 51 << 20
 F32 = jnp.float32
@@ -59,7 +58,7 @@
 
 
 def pack_kernel(
-    at_ref, src_ref, diag_hbm, pair_ref, cross_ref, even_ref, odd_ref, edge_ref, diag_ref, win, sems
+    at_ref, src_ref, diag_hbm, cross_ref, even_ref, odd_ref, edge_ref, diag_ref, win, sems
 ):
     mine = at_ref[0]
     other = jnp.where(mine >= 64, mine - 64, mine + 64)
@@ -84,12 +83,12 @@
     base = 0
     for d in range(1, PLANES + 1):
         count = WIDE - 2 * d
-        for dst_ref, at, right in ((pair_ref, mine, core == 0), (cross_ref, at_ref[1], core == 1)):
-            plane = jnp.where(right, PLANES - d, d - 1)
-            send(dst_ref, base, at, plane, d, count)
-            dst_ref[pl.ds(SEND_B + (d - 1) * 24, 24), :] = edge_ref[
-                plane, pl.ds(16 + at - DEPTH + d, 24), :
-            ]
+        at = at_ref[1]
+        plane = jnp.where(core == 1, PLANES - d, d - 1)
+        send(cross_ref, base, at, plane, d, count)
+        cross_ref[pl.ds(SEND_B + (d - 1) * 24, 24), :] = edge_ref[
+            plane, pl.ds(16 + at - DEPTH + d, 24), :
+        ]
         base += count * COLS
     for dst_ref, at, right in ((even_ref, mine, odd == 0), (odd_ref, other, odd == 1)):
         plane = jnp.where(right, PLANES - 1, 0)
@@ -103,12 +102,11 @@
         pack_kernel,
         out_shape=(
             out(SEND_B + SEND_E),
-            out(SEND_B + SEND_E),
             out(FAR_B + ROWS),
             out(FAR_B + ROWS),
         ),
         in_specs=[SMEM, ANY, ANY],
-        out_specs=(VMEM,) * 4,
+        out_specs=(VMEM,) * 3,
         scratch_shapes=[
             pltpu.VMEM((PLANES, 160, LANES), F32),
             pltpu.VMEM((PLANES, 128, LANES), F32),
@@ -120,7 +118,9 @@
     )(at, inputs, diagonal)
 
 
-def prep_kernel(at_ref, src_ref, diag_ref, obs_ref, after_ref, own_ref, probe_ref, edge_ref, win, obs, sems):
+def prep_kernel(
+    at_ref, src_ref, diag_ref, obs_ref, after_ref, own_ref, probe_ref, pair_ref, edge_ref, win, obs, sems
+):
     mine = at_ref[0]
     copies = window_copies(src_ref, first_row(mine), win, sems)
     copies.append(
@@ -135,6 +135,17 @@
         c.wait()
     flat = win.reshape(COLS * PLANES * 32, LANES)
     seen = obs.reshape(COLS * PLANES * ROWS, LANES)
+    base = 0
+    for d in range(1, PLANES + 1):
+        count = WIDE - 2 * d
+        plane = jnp.where(at_ref[2] == 0, PLANES - d, d - 1)
+        turned_rows(
+            pair_ref, base, flat, plane * 32 - first_row(mine), mine - DEPTH + d, count
+        )
+        pair_ref[pl.ds(SEND_B + (d - 1) * 24, 24), :] = edge_ref[
+            plane, pl.ds(16 + mine - DEPTH + d, 24), :
+        ]
+        base += count * COLS
     for x in range(PLANES):
         offset = x * 32 - first_row(mine)
         turned_rows(own_ref, x * WIDE * COLS, flat, offset, mine - DEPTH, WIDE)
@@ -153,9 +164,10 @@
         out_shape=(
             jax.ShapeDtypeStruct((OWN_B + PLANES * 32, LANES), F32),
             jax.ShapeDtypeStruct((32, PLANES * ROWS * LANES), BF16),
+            jax.ShapeDtypeStruct((SEND_B + SEND_E, LANES), F32),
         ),
         in_specs=[SMEM, ANY, VMEM, ANY, ANY],
-        out_specs=(VMEM, VMEM),
+        out_specs=(VMEM, VMEM, VMEM),
         scratch_shapes=[
             pltpu.VMEM((PLANES, 160, LANES), F32),
             pltpu.VMEM((COLS, PLANES, 32, LANES), F32),
@@ -564,11 +576,11 @@
     core, odd = row % 2, (row // 2) % 2
     other = jnp.where(core == odd, node ^ 4, node)
     at = jnp.stack([16 * node, 16 * other, core, odd]).astype(jnp.int32)
-    s1, s2, s3, s4 = pack(at, inputs, diagonal)
-    own, probe = prep(at, inputs, diagonal, observations, s3)
+    s2, s3, s4 = pack(at, inputs, diagonal)
     cross = swap_rows(s2, 1, lambda r: r % 2 == 1)
     far_even = swap_rows(s3, 2, lambda r: (r // 2) % 2 == 0)
     far_odd = swap_rows(s4, 2, lambda r: (r // 2) % 2 == 1)
+    own, probe, s1 = prep(at, inputs, diagonal, observations, s3)
     pair = swap_core(s1)
     fields, part = solve(at, frequencies, counts, own, pair, cross, far_even, far_odd, probe)
     total = xor_sum(part, "row", 16, [1, 2])

time: 138 us -> 141 us (1.022)
  waiting for transfers between devices: 33.1 us -> 37.4 us
    ppermute x3, waiting for transfers between devices: 7.3 us -> 11.7 us  [swap_rows(): return lax.ppermute(v, ('node', 'row'), both_ways(pairs))]
  transfers between devices with their start and end apart: 23 -> 23, of which waited for: 12 -> 12; matrix products, arithmetic and copies ran while one was open for 1% -> 1% of each run, Pallas kernels for 4% -> 2%
where the time goes in v1:
time: 141 us; the launch traced here: 139 us
  Pallas kernels  59.7 us (42%)
  waiting for transfers between devices  37.4 us (27%)
  starting transfers between devices  37.1 us (26%)
  local copies, waits for them, and re-layouts  3.2 us (2%)
    pallas_call x1, Pallas kernels, solve(): pl.pallas_call(solve_kernel, out_shape=(jax.ShapeDtypeStruct((QUAD * 64,...  42.3 us
    ppermute x10, starting transfers between devices, xor_sum(): lax.ppermute(x, axis, [(i, i ^ c) for i in range(size)])  16.9 us
    ppermute x6, waiting for transfers between devices, turn(): return lax.ppermute(v, 'node', [(i, i ^ mask) for i in range(8)])  12 us
    ppermute x3, waiting for transfers between devices, swap_rows(): return lax.ppermute(v, ('node', 'row'), both_ways(pairs))  11.7 us
    ppermute x10, waiting for transfers between devices, xor_sum(): lax.ppermute(x, axis, [(i, i ^ c) for i in range(size)])  11 us
    ppermute x3, starting transfers between devices, across(): return lax.ppermute(v, 'node', [(i, i ^ 4) for i in range(8)])  9.22 us
    ppermute x6, starting transfers between devices, turn(): return lax.ppermute(v, 'node', [(i, i ^ mask) for i in range(8)])  6.23 us
    pallas_call x1, Pallas kernels, respond(): pl.pallas_call(respond_kernel, out_shape=(jax.ShapeDtypeStruct((16, PLANE...  5.19 us
  transfers between devices with their start and end apart: 23, of which 12 were waited for; matrix products, arithmetic and copies ran while one was open for 1% of the time, Pallas kernels for 2%

profile of v1, /device:TPU:6, one launch (start us, length us, event | category | flops | bytes accessed | tf_op | source)
XLA Modules:
  0.0 138.6 jit_solution(12266860536890385793)
XLA Ops:
  0.7 0.1 pad_add_fusion.at_ref
  0.7 0.9 copy-done
  1.7 3.4 %pack.1 = (f32[1440,128]{1,0:T(8,128)S(1)}, f32[272,128]{1,0:T(8,128)S(1)}, f32[272,128]{1,0:T(8,128)S(1)}) custom-call(s32[4]{0:T(128)S(1)} %pad_add_fusion.at_ref, f32[16,4,128,128]{3,2,1,0:T(8,128)} %src_ref.3, f32[4,128,128]{2,1,0:T(8,128)S(1)} %copy-done), custom_call_target="tpu_custom_call" | custom-call | tf_op jit(solution)/shard_map/pack/pallas_call | solution.py:101
  5.1 0.0 copy-start.2
  5.1 0.0 copy-start.3
  5.1 0.0 copy-start.5
  5.1 0.0 copy-start.4
  5.1 4.0 %prep.1 = (f32[1792,128]{1,0:T(8,128)S(1)}, bf16[32,8192]{1,0:T(8,128)(2,1)S(1)}, f32[1440,128]{1,0:T(8,128)S(1)}) custom-call(s32[4]{0:T(128)S(1)} %pad_add_fusion.at_ref, f32[16,4,128,128]{3,2,1,0:T(8,128)} %src_ref.3, f32[4,128,128]{2,1,0:T(8,128)S(1)} %copy-done, f32[16,4,128,128]{3,2,1,0:T(8,128)} %obs_ref.1, f32[272,128]{1,0:T(8,128)S(1)} %get-tuple-element.12.after_ref), custom_call_target="tpu_custom_call" | custom-call | flops 40000000 | bytes 4000000 | tf_op jit(solution)/shard_map/prep/pallas_call | solution.py:162
  9.1 0.0 copy-start.1
  9.1 0.9 copy-done.1
  10.1 0.0 collective-permute-start
  10.1 0.7 collective-permute-start.1
  10.8 3.4 %collective-permute-start.2 = (f32[272,128]{1,0:T(8,128)S(1)}, f32[272,128]{1,0:T(8,128)S(1)}, u32[]{:S(2)}, u32[]{:S(2)}) collective-permute-start(f32[272,128]{1,0:T(8,128)S(1)} %get-tuple-element.12.after_ref), channel_id=1, source_target_pairs={{0,2},{1,3},{4,6},{5,7},{8,10},{9,11},{12,14},{13,15},{16,18},{17,... | collective-permute-start | bytes 417800 | tf_op jit(solution)/shard_map/ppermute | solution.py:503
  14.2 0.7 collective-permute-start.3
  14.8 11.7 %collective-permute-done.2.even_ref = f32[272,128]{1,0:T(8,128)S(1)} collective-permute-done((f32[272,128]{1,0:T(8,128)S(1)}, f32[272,128]{1,0:T(8,128)S(1)}, u32[]{:S(2)}, u32[]{:S(2)}) %collective-permute-start.2) | collective-permute-done | bytes 139296 | tf_op jit(solution)/shard_map/ppermute | solution.py:503
  26.5 0.0 collective-permute-done.3.odd_ref
  26.5 0.0 collective-permute-done.pair_ref
  26.5 0.0 collective-permute-done.1.cross_ref
  26.5 0.0 copy-done.2
  26.5 42.3 %solve.1 = (bf16[512,8192]{1,0:T(8,128)(2,1)}, f32[48,128]{1,0:T(8,128)S(1)}) custom-call(s32[4]{0:T(128)S(1)} %pad_add_fusion.at_ref, f32[8]{0:T(128)S(1)} %copy-done.2, s32[8]{0:T(128)S(1)} %copy-done.3, f32[1792,128]{1,0:T(8,128)} %copy-done.1, f32[1440,128]{1,0:T(8,128)S(1)} %collective-permute-done.pair_ref, ...), custom_call_target="tpu_custom_call" | custom-call | tf_op jit(solution)/shard_map/solve/pallas_call | solution.py:388
  68.8 0.1 collective-permute-start.4
  68.9 2.9 %collective-permute-start.5 = (f32[48,128]{1,0:T(8,128)S(1)}, f32[48,128]{1,0:T(8,128)S(1)}, u32[]{:S(2)}, u32[]{:S(2)}) collective-permute-start(f32[48,128]{1,0:T(8,128)S(1)} %get-tuple-element.18), channel_id=1, source_target_pairs={{0,2},{1,3},{2,0},{3,1},{4,6},{5,7},{6,4},{7,5},{8,10},{9,11},{10,... | collective-permute-start | bytes 73736 | tf_op jit(solution)/shard_map/ppermute | solution.py:510
  71.8 0.0 collective-permute-start.6
  71.8 0.0 collective-permute-done.4
  71.8 1.8 %collective-permute-done.5 = f32[48,128]{1,0:T(8,128)S(1)} collective-permute-done((f32[48,128]{1,0:T(8,128)S(1)}, f32[48,128]{1,0:T(8,128)S(1)}, u32[]{:S(2)}, u32[]{:S(2)}) %collective-permute-start.5) | collective-permute-done | bytes 24608 | tf_op jit(solution)/shard_map/ppermute | solution.py:510
  73.6 1.4 %collective-permute-done.6 = f32[48,128]{1,0:T(8,128)S(1)} collective-permute-done((f32[48,128]{1,0:T(8,128)S(1)}, f32[48,128]{1,0:T(8,128)S(1)}, u32[]{:S(2)}, u32[]{:S(2)}) %collective-permute-start.6) | collective-permute-done | bytes 24608 | tf_op jit(solution)/shard_map/ppermute | solution.py:510
  75.1 1.8 %collective-permute-start.7 = (f32[48,128]{1,0:T(8,128)S(1)}, f32[48,128]{1,0:T(8,128)S(1)}, u32[]{:S(2)}, u32[]{:S(2)}) collective-permute-start(f32[48,128]{1,0:T(8,128)S(1)} %add_add_fusion.2), channel_id=1, source_target_pairs={{0,4},{1,5},{2,6},{3,7},{4,0},{5,1},{6,2},{7,3},{8,12},{9,13},{10,... | collective-permute-start | bytes 73736 | tf_op jit(solution)/shard_map/ppermute | solution.py:510
  76.9 2.4 %collective-permute-start.8 = (f32[48,128]{1,0:T(8,128)S(1)}, f32[48,128]{1,0:T(8,128)S(1)}, u32[]{:S(2)}, u32[]{:S(2)}) collective-permute-start(f32[48,128]{1,0:T(8,128)S(1)} %add_add_fusion.2), channel_id=1, source_target_pairs={{0,8},{1,9},{2,10},{3,11},{4,12},{5,13},{6,14},{7,15},{8,0},{9,1},... | collective-permute-start | bytes 73736 | tf_op jit(solution)/shard_map/ppermute | solution.py:510
  79.3 0.7 collective-permute-start.9
  80.0 0.0 collective-permute-done.7
  80.0 2.2 %collective-permute-done.8 = f32[48,128]{1,0:T(8,128)S(1)} collective-permute-done((f32[48,128]{1,0:T(8,128)S(1)}, f32[48,128]{1,0:T(8,128)S(1)}, u32[]{:S(2)}, u32[]{:S(2)}) %collective-permute-start.8) | collective-permute-done | bytes 24608 | tf_op jit(solution)/shard_map/ppermute | solution.py:510
  82.2 2.1 %collective-permute-done.9 = f32[48,128]{1,0:T(8,128)S(1)} collective-permute-done((f32[48,128]{1,0:T(8,128)S(1)}, f32[48,128]{1,0:T(8,128)S(1)}, u32[]{:S(2)}, u32[]{:S(2)}) %collective-permute-start.9) | collective-permute-done | bytes 24608 | tf_op jit(solution)/shard_map/ppermute | solution.py:510
  84.4 0.9 collective-permute-start.10
  85.3 1.1 collective-permute-start.11
  86.4 2.8 %collective-permute-start.12 = (f32[48,128]{1,0:T(8,128)S(1)}, f32[48,128]{1,0:T(8,128)S(1)}, u32[]{:S(2)}, u32[]{:S(2)}) collective-permute-start(f32[48,128]{1,0:T(8,128)S(1)} %add_add_fusion.1), channel_id=1, source_target_pairs={{0,48},{16,32},{32,16},{48,0},{64,112},{80,96},{96,80},{112,64},{1... | collective-permute-start | bytes 73736 | tf_op jit(solution)/shard_map/ppermute | solution.py:510
  89.1 0.0 collective-permute-done.10
  89.1 1.5 %collective-permute-done.11 = f32[48,128]{1,0:T(8,128)S(1)} collective-permute-done((f32[48,128]{1,0:T(8,128)S(1)}, f32[48,128]{1,0:T(8,128)S(1)}, u32[]{:S(2)}, u32[]{:S(2)}) %collective-permute-start.11) | collective-permute-done | bytes 24608 | tf_op jit(solution)/shard_map/ppermute | solution.py:510
  90.6 0.8 collective-permute-done.12
  91.4 4.2 %collective-permute-start.13 = (f32[48,128]{1,0:T(8,128)S(1)}, f32[48,128]{1,0:T(8,128)S(1)}, u32[]{:S(2)}, u32[]{:S(2)}) collective-permute-start(f32[48,128]{1,0:T(8,128)S(1)} %add_add_fusion), channel_id=1, source_target_pairs={{0,64},{16,80},{32,96},{48,112},{64,0},{80,16},{96,32},{112,48},{1... | collective-permute-start | bytes 73736 | tf_op jit(solution)/shard_map/ppermute | solution.py:510
  95.6 0.6 dynamic_slice.3.pick_ref
  96.2 1.2 collective-permute-done.13
  97.4 5.2 %respond.1 = (f32[16,4,16,128]{3,2,1,0:T(8,128)S(1)}, f32[16,128]{1,0:T(8,128)S(1)}) custom-call(s32[1]{0:T(128)} %dynamic_slice.3.pick_ref, f32[8]{0:T(128)S(1)} %copy-done.4, f32[48,128]{1,0:T(8,128)S(1)} %add.90.sum_ref, bf16[512,8192]{1,0:T(8,128)(2,1)} %get-tuple-element.19.full_ref), custom_call_target="tpu_custom_call" | custom-call | tf_op jit(solution)/shard_map/respond/pallas_call | solution.py:470
  102.6 2.8 %collective-permute-start.17 = (f32[16,4,16,128]{3,2,1,0:T(8,128)S(1)}, f32[16,4,16,128]{3,2,1,0:T(8,128)S(1)}, u32[]{:S(2)}, u32[]{:S(2)}) collective-permute-start(f32[16,4,16,128]{3,2,1,0:T(8,128)S(1)} %get-tuple-element.20.refs_0_), channel_id=1, source_target_pairs={{0,48},{16,32},{32,16},{48,0},{64,112},{80,96},{96,80},{112,64},{1... | collective-permute-start | bytes 1572872 | tf_op jit(solution)/shard_map/ppermute | solution.py:517
  105.5 0.0 collective-permute-start.20
  105.5 3.5 %collective-permute-start.14 = (f32[16,4,16,128]{3,2,1,0:T(8,128)S(1)}, f32[16,4,16,128]{3,2,1,0:T(8,128)S(1)}, u32[]{:S(2)}, u32[]{:S(2)}) collective-permute-start(f32[16,4,16,128]{3,2,1,0:T(8,128)S(1)} %get-tuple-element.20.refs_0_), channel_id=1, source_target_pairs={{0,64},{16,80},{32,96},{48,112},{64,0},{80,16},{96,32},{112,48},{1... | collective-permute-start | bytes 1572872 | tf_op jit(solution)/shard_map/ppermute | solution.py:521
  109.0 5.0 %collective-permute-done.17.refs_2_ = f32[16,4,16,128]{3,2,1,0:T(8,128)S(1)} collective-permute-done((f32[16,4,16,128]{3,2,1,0:T(8,128)S(1)}, f32[16,4,16,128]{3,2,1,0:T(8,128)S(1)}, u32[]{:S(2)}, u32[]{:S(2)}) %collective-permute-start.17) | collective-permute-done | bytes 524320 | tf_op jit(solution)/shard_map/ppermute | solution.py:517
  114.0 0.1 collective-permute-start.18
  114.1 4.7 %collective-permute-done.20.refs_1_ = f32[16,4,16,128]{3,2,1,0:T(8,128)S(1)} collective-permute-done((f32[16,4,16,128]{3,2,1,0:T(8,128)S(1)}, f32[16,4,16,128]{3,2,1,0:T(8,128)S(1)}, u32[]{:S(2)}, u32[]{:S(2)}) %collective-permute-start.20) | collective-permute-done | bytes 524320 | tf_op jit(solution)/shard_map/ppermute | solution.py:517
  118.8 0.1 collective-permute-start.21
  118.9 0.0 collective-permute-done.14.refs_3_
  119.0 0.4 collective-permute-start.15
  119.3 2.9 %collective-permute-start.16 = (f32[16,4,16,128]{3,2,1,0:T(8,128)S(1)}, f32[16,4,16,128]{3,2,1,0:T(8,128)S(1)}, u32[]{:S(2)}, u32[]{:S(2)}) collective-permute-start(f32[16,4,16,128]{3,2,1,0:T(8,128)S(1)} %collective-permute-done.14.refs_3_), channel_id=1, source_target_pairs={{0,48},{16,32},{32,16},{48,0},{64,112},{80,96},{96,80},{112,64},{1... | collective-permute-start | bytes 1572872 | tf_op jit(solution)/shard_map/ppermute | solution.py:517
  122.2 2.3 %collective-permute-done.18.refs_4_ = f32[8,4,16,128]{3,2,1,0:T(8,128)S(1)} collective-permute-done((f32[8,4,16,128]{3,2,1,0:T(8,128)S(1)}, f32[8,4,16,128]{3,2,1,0:T(8,128)S(1)}, u32[]{:S(2)}, u32[]{:S(2)}) %collective-permute-start.18) | collective-permute-done | bytes 262176 | tf_op jit(solution)/shard_map/ppermute | solution.py:517
  124.4 3.5 %collective-permute-start.19 = (f32[8,4,16,128]{3,2,1,0:T(8,128)S(1)}, f32[8,4,16,128]{3,2,1,0:T(8,128)}, u32[]{:S(2)}, u32[]{:S(2)}) collective-permute-start(f32[8,4,16,128]{3,2,1,0:T(8,128)S(1)} %collective-permute-done.18.refs_4_), channel_id=1, source_target_pairs={{0,64},{16,80},{32,96},{48,112},{64,0},{80,16},{96,32},{112,48},{1... | collective-permute-start | bytes 786440 | tf_op jit(solution)/shard_map/ppermute | solution.py:521
  128.0 0.0 collective-permute-done.21.refs_5_
  128.0 2.2 %collective-permute-start.22 = (f32[8,4,16,128]{3,2,1,0:T(8,128)}, f32[8,4,16,128]{3,2,1,0:T(8,128)}, u32[]{:S(2)}, u32[]{:S(2)}) collective-permute-start(f32[8,4,16,128]{3,2,1,0:T(8,128)} %collective-permute-done.21.refs_5_), channel_id=1, source_target_pairs={{0,64},{16,80},{32,96},{48,112},{64,0},{80,16},{96,32},{112,48},{1... | collective-permute-start | bytes 786440 | tf_op jit(solution)/shard_map/ppermute | solution.py:521
  130.1 0.1 stack.50.spot_ref
  130.2 0.6 slice_bitcast_fusion
  130.8 2.6 %early.1.refs_4_ = f32[16,4,128,128]{3,2,1,0:T(8,128)} custom-call(s32[8]{0:T(128)S(1)} %stack.50.spot_ref, f32[16,4,16,128]{3,2,1,0:T(8,128)S(1)} %get-tuple-element.20.refs_0_, f32[16,4,16,128]{3,2,1,0:T(8,128)S(1)} %collective-permute-done.20.refs_1_, f32[16,4,16,128]{3,2,1,0:T(8,128)S(1)} %collective-permute-done.17.refs_2_, ...), custom_call_target="tpu_custom_call" | custom-call | tf_op jit(solution)/shard_map/early/pallas_call | solution.py:552
  133.4 0.0 collective-permute-done.19.refs_2_
  133.5 2.7 %collective-permute-done.22.refs_3_ = f32[8,4,16,128]{3,2,1,0:T(8,128)} collective-permute-done((f32[8,4,16,128]{3,2,1,0:T(8,128)}, f32[8,4,16,128]{3,2,1,0:T(8,128)}, u32[]{:S(2)}, u32[]{:S(2)}) %collective-permute-start.22) | collective-permute-done | bytes 262176 | tf_op jit(solution)/shard_map/ppermute | solution.py:521
  136.2 0.0 collective-permute-done.15.refs_0_
  136.2 0.0 collective-permute-done.16.refs_1_
  136.2 2.3 %late.1 = f32[16,4,128,128]{3,2,1,0:T(8,128)} custom-call(s32[8]{0:T(128)S(1)} %stack.50.spot_ref, f32[16,4,16,128]{3,2,1,0:T(8,128)S(1)} %collective-permute-done.15.refs_0_, f32[16,4,16,128]{3,2,1,0:T(8,128)S(1)} %collective-permute-done.16.refs_1_, f32[8,4,16,128]{3,2,1,0:T(8,128)} %collective-permute-done.19.refs_2_, ...), custom_call_target="tpu_custom_call", output_to_operand_aliasing={{}: (5, {})} | custom-call | tf_op jit(solution)/shard_map/late/pallas_call | solution.py:561
  (10 shorter events, 0.1 us)
Async XLA Ops:
  0.7 1.0 copy-start
  5.1 21.4 %copy-start.2 = (f32[8]{0:T(128)S(1)}, f32[8]{0:T(128)}, u32[]{:S(2)}) copy-start(f32[8]{0:T(128)} %freq_ref.1) | copy-start | bytes 100
  5.1 21.4 %copy-start.3 = (s32[8]{0:T(128)S(1)}, s32[8]{0:T(128)}, u32[]{:S(2)}) copy-start(s32[8]{0:T(128)} %count_ref.1) | copy-start | bytes 100
  5.1 90.5 %copy-start.5 = (s32[8]{0:T(128)S(1)}, s32[8]{0:T(128)}, u32[]{:S(2)}) copy-start(s32[8]{0:T(128)} %param.13) | copy-start | bytes 100
  5.1 92.3 %copy-start.4 = (f32[8]{0:T(128)S(1)}, f32[8]{0:T(128)}, u32[]{:S(2)}) copy-start(f32[8]{0:T(128)} %weight_ref.1) | copy-start | bytes 100
  9.1 0.9 copy-start.1
  10.1 16.5 %collective-permute-start = (f32[1440,128]{1,0:T(8,128)S(1)}, f32[1440,128]{1,0:T(8,128)S(1)}, u32[]{:S(2)}, u32[]{:S(2)}) collective-permute-start(f32[1440,128]{1,0:T(8,128)S(1)} %get-tuple-element.14), channel_id=1, source_target_pairs={{0,1},{1,0},{2,3},{3,2},{4,5},{5,4},{6,7},{7,6},{8,9},{9,8},{10,11... | collective-permute-start | bytes 2211848 | tf_op jit(solution)/shard_map/ppermute | solution.py:493
  10.1 16.5 %collective-permute-start.1 = (f32[1440,128]{1,0:T(8,128)S(1)}, f32[1440,128]{1,0:T(8,128)S(1)}, u32[]{:S(2)}, u32[]{:S(2)}) collective-permute-start(f32[1440,128]{1,0:T(8,128)S(1)} %get-tuple-element.15), channel_id=1, source_target_pairs={{1,2},{3,68},{5,6},{7,72},{9,10},{11,76},{13,14},{17,18},{19,84},{... | collective-permute-start | bytes 2211848 | tf_op jit(solution)/shard_map/ppermute | solution.py:503
  10.8 15.7 %collective-permute-start.2 = (f32[272,128]{1,0:T(8,128)S(1)}, f32[272,128]{1,0:T(8,128)S(1)}, u32[]{:S(2)}, u32[]{:S(2)}) collective-permute-start(f32[272,128]{1,0:T(8,128)S(1)} %get-tuple-element.12.after_ref), channel_id=1, source_target_pairs={{0,2},{1,3},{4,6},{5,7},{8,10},{9,11},{12,14},{13,15},{16,18},{17,... | collective-permute-start | bytes 417800 | tf_op jit(solution)/shard_map/ppermute | solution.py:503
  14.2 12.3 %collective-permute-start.3 = (f32[272,128]{1,0:T(8,128)S(1)}, f32[272,128]{1,0:T(8,128)S(1)}, u32[]{:S(2)}, u32[]{:S(2)}) collective-permute-start(f32[272,128]{1,0:T(8,128)S(1)} %get-tuple-element.16), channel_id=1, source_target_pairs={{2,68},{3,69},{6,72},{7,73},{10,76},{11,77},{18,84},{19,85},{22,88... | collective-permute-start | bytes 417800 | tf_op jit(solution)/shard_map/ppermute | solution.py:503
  68.8 3.0 %collective-permute-start.4 = (f32[48,128]{1,0:T(8,128)S(1)}, f32[48,128]{1,0:T(8,128)S(1)}, u32[]{:S(2)}, u32[]{:S(2)}) collective-permute-start(f32[48,128]{1,0:T(8,128)S(1)} %get-tuple-element.18), channel_id=1, source_target_pairs={{0,1},{1,0},{2,3},{3,2},{4,5},{5,4},{6,7},{7,6},{8,9},{9,8},{10,11... | collective-permute-start | bytes 73736 | tf_op jit(solution)/shard_map/ppermute | solution.py:510
  68.9 4.7 %collective-permute-start.5 = (f32[48,128]{1,0:T(8,128)S(1)}, f32[48,128]{1,0:T(8,128)S(1)}, u32[]{:S(2)}, u32[]{:S(2)}) collective-permute-start(f32[48,128]{1,0:T(8,128)S(1)} %get-tuple-element.18), channel_id=1, source_target_pairs={{0,2},{1,3},{2,0},{3,1},{4,6},{5,7},{6,4},{7,5},{8,10},{9,11},{10,... | collective-permute-start | bytes 73736 | tf_op jit(solution)/shard_map/ppermute | solution.py:510
  71.8 3.3 %collective-permute-start.6 = (f32[48,128]{1,0:T(8,128)S(1)}, f32[48,128]{1,0:T(8,128)S(1)}, u32[]{:S(2)}, u32[]{:S(2)}) collective-permute-start(f32[48,128]{1,0:T(8,128)S(1)} %get-tuple-element.18), channel_id=1, source_target_pairs={{0,3},{1,2},{2,1},{3,0},{4,7},{5,6},{6,5},{7,4},{8,11},{9,10},{10,... | collective-permute-start | bytes 73736 | tf_op jit(solution)/shard_map/ppermute | solution.py:510
  75.1 5.0 %collective-permute-start.7 = (f32[48,128]{1,0:T(8,128)S(1)}, f32[48,128]{1,0:T(8,128)S(1)}, u32[]{:S(2)}, u32[]{:S(2)}) collective-permute-start(f32[48,128]{1,0:T(8,128)S(1)} %add_add_fusion.2), channel_id=1, source_target_pairs={{0,4},{1,5},{2,6},{3,7},{4,0},{5,1},{6,2},{7,3},{8,12},{9,13},{10,... | collective-permute-start | bytes 73736 | tf_op jit(solution)/shard_map/ppermute | solution.py:510
  76.9 5.3 %collective-permute-start.8 = (f32[48,128]{1,0:T(8,128)S(1)}, f32[48,128]{1,0:T(8,128)S(1)}, u32[]{:S(2)}, u32[]{:S(2)}) collective-permute-start(f32[48,128]{1,0:T(8,128)S(1)} %add_add_fusion.2), channel_id=1, source_target_pairs={{0,8},{1,9},{2,10},{3,11},{4,12},{5,13},{6,14},{7,15},{8,0},{9,1},... | collective-permute-start | bytes 73736 | tf_op jit(solution)/shard_map/ppermute | solution.py:510
  79.3 5.0 %collective-permute-start.9 = (f32[48,128]{1,0:T(8,128)S(1)}, f32[48,128]{1,0:T(8,128)S(1)}, u32[]{:S(2)}, u32[]{:S(2)}) collective-permute-start(f32[48,128]{1,0:T(8,128)S(1)} %add_add_fusion.2), channel_id=1, source_target_pairs={{0,12},{1,13},{2,14},{3,15},{4,8},{5,9},{6,10},{7,11},{8,4},{9,5},... | collective-permute-start | bytes 73736 | tf_op jit(solution)/shard_map/ppermute | solution.py:510
  84.4 4.8 %collective-permute-start.10 = (f32[48,128]{1,0:T(8,128)S(1)}, f32[48,128]{1,0:T(8,128)S(1)}, u32[]{:S(2)}, u32[]{:S(2)}) collective-permute-start(f32[48,128]{1,0:T(8,128)S(1)} %add_add_fusion.1), channel_id=1, source_target_pairs={{0,16},{16,0},{32,48},{48,32},{64,80},{80,64},{96,112},{112,96},{1... | collective-permute-start | bytes 73736 | tf_op jit(solution)/shard_map/ppermute | solution.py:510
  85.3 5.3 %collective-permute-start.11 = (f32[48,128]{1,0:T(8,128)S(1)}, f32[48,128]{1,0:T(8,128)S(1)}, u32[]{:S(2)}, u32[]{:S(2)}) collective-permute-start(f32[48,128]{1,0:T(8,128)S(1)} %add_add_fusion.1), channel_id=1, source_target_pairs={{0,32},{16,48},{32,0},{48,16},{64,96},{80,112},{96,64},{112,80},{1... | collective-permute-start | bytes 73736 | tf_op jit(solution)/shard_map/ppermute | solution.py:510
  86.4 5.0 %collective-permute-start.12 = (f32[48,128]{1,0:T(8,128)S(1)}, f32[48,128]{1,0:T(8,128)S(1)}, u32[]{:S(2)}, u32[]{:S(2)}) collective-permute-start(f32[48,128]{1,0:T(8,128)S(1)} %add_add_fusion.1), channel_id=1, source_target_pairs={{0,48},{16,32},{32,16},{48,0},{64,112},{80,96},{96,80},{112,64},{1... | collective-permute-start | bytes 73736 | tf_op jit(solution)/shard_map/ppermute | solution.py:510
  91.4 6.0 %collective-permute-start.13 = (f32[48,128]{1,0:T(8,128)S(1)}, f32[48,128]{1,0:T(8,128)S(1)}, u32[]{:S(2)}, u32[]{:S(2)}) collective-permute-start(f32[48,128]{1,0:T(8,128)S(1)} %add_add_fusion), channel_id=1, source_target_pairs={{0,64},{16,80},{32,96},{48,112},{64,0},{80,16},{96,32},{112,48},{1... | collective-permute-start | bytes 73736 | tf_op jit(solution)/shard_map/ppermute | solution.py:510
  102.6 11.4 %collective-permute-start.17 = (f32[16,4,16,128]{3,2,1,0:T(8,128)S(1)}, f32[16,4,16,128]{3,2,1,0:T(8,128)S(1)}, u32[]{:S(2)}, u32[]{:S(2)}) collective-permute-start(f32[16,4,16,128]{3,2,1,0:T(8,128)S(1)} %get-tuple-element.20.refs_0_), channel_id=1, source_target_pairs={{0,48},{16,32},{32,16},{48,0},{64,112},{80,96},{96,80},{112,64},{1... | collective-permute-start | bytes 1572872 | tf_op jit(solution)/shard_map/ppermute | solution.py:517
  105.5 13.4 %collective-permute-start.20 = (f32[16,4,16,128]{3,2,1,0:T(8,128)S(1)}, f32[16,4,16,128]{3,2,1,0:T(8,128)S(1)}, u32[]{:S(2)}, u32[]{:S(2)}) collective-permute-start(f32[16,4,16,128]{3,2,1,0:T(8,128)S(1)} %get-tuple-element.20.refs_0_), channel_id=1, source_target_pairs={{0,16},{16,0},{32,48},{48,32},{64,80},{80,64},{96,112},{112,96},{1... | collective-permute-start | bytes 1572872 | tf_op jit(solution)/shard_map/ppermute | solution.py:517
  105.5 13.5 %collective-permute-start.14 = (f32[16,4,16,128]{3,2,1,0:T(8,128)S(1)}, f32[16,4,16,128]{3,2,1,0:T(8,128)S(1)}, u32[]{:S(2)}, u32[]{:S(2)}) collective-permute-start(f32[16,4,16,128]{3,2,1,0:T(8,128)S(1)} %get-tuple-element.20.refs_0_), channel_id=1, source_target_pairs={{0,64},{16,80},{32,96},{48,112},{64,0},{80,16},{96,32},{112,48},{1... | collective-permute-start | bytes 1572872 | tf_op jit(solution)/shard_map/ppermute | solution.py:521
  114.0 10.4 %collective-permute-start.18 = (f32[8,4,16,128]{3,2,1,0:T(8,128)S(1)}, f32[8,4,16,128]{3,2,1,0:T(8,128)S(1)}, u32[]{:S(2)}, u32[]{:S(2)}) collective-permute-start(f32[8,4,16,128]{3,2,1,0:T(8,128)S(1)} %slice.12), channel_id=1, source_target_pairs={{0,16},{16,0},{32,48},{48,32},{64,80},{80,64},{96,112},{112,96},{1... | collective-permute-start | bytes 786440 | tf_op jit(solution)/shard_map/ppermute | solution.py:517
  118.8 9.1 %collective-permute-start.21 = (f32[8,4,16,128]{3,2,1,0:T(8,128)S(1)}, f32[8,4,16,128]{3,2,1,0:T(8,128)}, u32[]{:S(2)}, u32[]{:S(2)}) collective-permute-start(f32[8,4,16,128]{3,2,1,0:T(8,128)S(1)} %slice.13), channel_id=1, source_target_pairs={{0,48},{16,32},{32,16},{48,0},{64,112},{80,96},{96,80},{112,64},{1... | collective-permute-start | bytes 786440 | tf_op jit(solution)/shard_map/ppermute | solution.py:517
  119.0 17.2 %collective-permute-start.15 = (f32[16,4,16,128]{3,2,1,0:T(8,128)S(1)}, f32[16,4,16,128]{3,2,1,0:T(8,128)S(1)}, u32[]{:S(2)}, u32[]{:S(2)}) collective-permute-start(f32[16,4,16,128]{3,2,1,0:T(8,128)S(1)} %collective-permute-done.14.refs_3_), channel_id=1, source_target_pairs={{0,16},{16,0},{32,48},{48,32},{64,80},{80,64},{96,112},{112,96},{1... | collective-permute-start | bytes 1572872 | tf_op jit(solution)/shard_map/ppermute | solution.py:517
  119.3 16.9 %collective-permute-start.16 = (f32[16,4,16,128]{3,2,1,0:T(8,128)S(1)}, f32[16,4,16,128]{3,2,1,0:T(8,128)S(1)}, u32[]{:S(2)}, u32[]{:S(2)}) collective-permute-start(f32[16,4,16,128]{3,2,1,0:T(8,128)S(1)} %collective-permute-done.14.refs_3_), channel_id=1, source_target_pairs={{0,48},{16,32},{32,16},{48,0},{64,112},{80,96},{96,80},{112,64},{1... | collective-permute-start | bytes 1572872 | tf_op jit(solution)/shard_map/ppermute | solution.py:517
  124.4 9.0 %collective-permute-start.19 = (f32[8,4,16,128]{3,2,1,0:T(8,128)S(1)}, f32[8,4,16,128]{3,2,1,0:T(8,128)}, u32[]{:S(2)}, u32[]{:S(2)}) collective-permute-start(f32[8,4,16,128]{3,2,1,0:T(8,128)S(1)} %collective-permute-done.18.refs_4_), channel_id=1, source_target_pairs={{0,64},{16,80},{32,96},{48,112},{64,0},{80,16},{96,32},{112,48},{1... | collective-permute-start | bytes 786440 | tf_op jit(solution)/shard_map/ppermute | solution.py:521
  128.0 8.2 %collective-permute-start.22 = (f32[8,4,16,128]{3,2,1,0:T(8,128)}, f32[8,4,16,128]{3,2,1,0:T(8,128)}, u32[]{:S(2)}, u32[]{:S(2)}) collective-permute-start(f32[8,4,16,128]{3,2,1,0:T(8,128)} %collective-permute-done.21.refs_5_), channel_id=1, source_target_pairs={{0,64},{16,80},{32,96},{48,112},{64,0},{80,16},{96,32},{112,48},{1... | collective-permute-start | bytes 786440 | tf_op jit(solution)/shard_map/ppermute | solution.py:521
